TPU v7x, 32 devices: a whole 2x2x4 slice. The times are simulated.
32 devices in a mesh: dp: 2 (over x), expert: 16 (over z, y, core).
Axes of the slice: x: 2, y: 2, z: 4, core: 2. Of those that a mesh axis runs over, the one named last changes fastest.
Arguments:
- tokens: bfloat16 [512, 2048], P('expert', 'dp'), may hold values from -6 to 6
- routes: int32 [512, 8], P('expert'), may hold values from 0 to 63, all different within a row; in each aligned block of 32 rows (0 to 31, 32 to 63, ...) at most 4 rows name the same one
- route_weight: float32 [512, 8], P('expert'), may hold values from 0.05 to 0.5
- gate_weight: bfloat16 [64, 2048, 768], P('expert', 'dp'), may hold values from -0.125 to 0.125
- up_weight: bfloat16 [64, 2048, 768], P('expert', 'dp'), may hold values from -0.125 to 0.125
- down_weight: bfloat16 [64, 768, 2048], P('expert', None, 'dp'), may hold values from -0.21875 to 0.21875
- trained_down: float32 [64, 768, 2048], P('expert', 'dp'), may hold values from -0.21875 to 0.21875
Outputs:
- mixed: bfloat16 [512, 2048], P('expert', 'dp')
- synced_down: bfloat16 [64, 768, 2048], P('expert', None, 'dp')
Inputs may be any that keep to these rules, and one draw needn't show every extreme that they name: `routes`: each row names 8 different experts. Among the 32 rows of one device (aligned blocks), no expert is named more than 4 times, a bound that some block reaches.
All inputs are finite; a program needn't handle non-finite values.
Results may differ from a plain program's by a relative error of at most 0.0058.
Values may be sent and summed in bfloat16 or wider, within the bound.
A program may use at most 128 MiB of HBM per device.

v0:
```python
import functools

import jax
import jax.numpy as jnp
from jax import lax
from jax.experimental import pallas as pl
from jax.experimental.pallas import tpu as pltpu
from jax.sharding import PartitionSpec as P

CAP = 4
CHUNK_BYTES = 200_000
EARLY = 1 / 4
MIDDLE = 3 / 16
MESH = pl.DeviceIdType.MESH


def fused(
    dims,
    tokens, routes, route_weight, gate_weight, up_weight, down_weight, trained,
    mixed, synced,
    tok_v, routes_v, weight_v, gate_v, up_v, down_v, wide, narrow,
    outgoing, arrived, by_expert, partial, to_send, peers_part, hidden,
    leaving, returned,
    small_sem, load_sem, wide_sem, sync_send, sync_recv,
    out_send, out_recv, part_send, part_recv, hid_send, hid_recv, ret_send, ret_recv,
):
    n, groups, el, rc, nsub = dims
    p, me = lax.axis_index("dp"), lax.axis_index("expert")
    rows = trained.shape[1]
    tok_rows, width = tok_v.shape
    ff = gate_v.shape[2]
    slots = el * CAP
    total = groups * slots
    share = total // n
    per_expert = total // el
    per_peer = el * nsub
    remote = (n - 1) * per_peer
    early = nsub + round(remote * EARLY)
    middle = early + round(remote * MIDDLE)

    def peer(offset):
        return lax.rem(p + offset, n)

    def share_of(device):
        return pl.ds(pl.multiple_of(device * share, 16), share)

    def chunk_at(i):
        offset = lax.rem(lax.div(i, per_peer) + 1, n)
        e = lax.rem(lax.div(i, nsub), el)
        return offset, e, lax.rem(i, nsub) * rc

    def load_wide(i):
        offset, e, r = chunk_at(i)
        cols = pl.ds(pl.multiple_of(peer(offset) * width, 128), width)
        return pltpu.make_async_copy(
            trained.at[e, pl.ds(pl.multiple_of(r, 16), rc), cols], wide.at[i], wide_sem.at[i]
        )

    def sync_copy(i):
        offset, e, r = chunk_at(i)
        return pltpu.make_async_remote_copy(
            src_ref=narrow.at[i],
            dst_ref=synced.at[e, pl.ds(pl.multiple_of(p * rows + r, 16), rc), :],
            send_sem=sync_send.at[i],
            recv_sem=sync_recv.at[i],
            device_id=(peer(offset), me),
            device_id_type=MESH,
        )

    def sync_arrival(i):
        offset, e, r = chunk_at(i)
        source = lax.rem(p + n - offset, n)
        return pltpu.make_async_remote_copy(
            src_ref=narrow.at[i],
            dst_ref=synced.at[e, pl.ds(pl.multiple_of(source * rows + r, 16), rc), :],
            send_sem=sync_send.at[i],
            recv_sem=sync_recv.at[i],
            device_id=(peer(offset), me),
            device_id_type=MESH,
        )

    def each(start, stop, body):
        def step(i, carry):
            body(i)
            return carry

        lax.fori_loop(start, stop, step, 0)

    def send_chunk(i):
        load_wide(i).wait()
        narrow[i] = wide[i].astype(jnp.bfloat16)
        sync_copy(i).start()

    def spread(source, target, send, recv, offset, slot):
        return pltpu.make_async_remote_copy(
            src_ref=source.at[slot],
            dst_ref=target.at[me],
            send_sem=send.at[offset],
            recv_sem=recv.at[offset],
            device_id=(p, slot),
            device_id_type=MESH,
        )

    def spread_all(source, target, send, recv):
        each(
            1, groups,
            lambda o: spread(source, target, send, recv, o, lax.rem(me + o, groups)).start(),
        )

    def gather_all(source, target, send, recv):
        def body(o):
            origin = lax.rem(me + groups - o, groups)
            pltpu.make_async_remote_copy(
                src_ref=source.at[origin],
                dst_ref=target.at[origin],
                send_sem=send.at[o],
                recv_sem=recv.at[o],
                device_id=(p, origin),
                device_id_type=MESH,
            ).wait_recv()

        each(1, groups, body)

    def part_copy(o):
        return pltpu.make_async_remote_copy(
            src_ref=to_send.at[peer(o)],
            dst_ref=peers_part.at[o],
            send_sem=part_send.at[o],
            recv_sem=part_recv.at[o],
            device_id=(peer(o), me),
            device_id_type=MESH,
        )

    def hidden_copy(o, origin):
        return pltpu.make_async_remote_copy(
            src_ref=hidden.at[share_of(origin), :],
            dst_ref=hidden.at[share_of(origin), :],
            send_sem=hid_send.at[o],
            recv_sem=hid_recv.at[o],
            device_id=(peer(o), me),
            device_id_type=MESH,
        )

    smalls = [
        pltpu.make_async_copy(src, dst, small_sem.at[i])
        for i, (src, dst) in enumerate(
            ((routes, routes_v), (route_weight, weight_v), (tokens, tok_v))
        )
    ]

    def weights(k, src, dst):
        return lambda e: pltpu.make_async_copy(src.at[e], dst.at[e], load_sem.at[k * el + e])

    load_gate = weights(0, gate_weight, gate_v)
    load_up = weights(1, up_weight, up_v)
    load_down = weights(2, down_weight, down_v)

    barrier = pltpu.get_barrier_semaphore()

    def greet(device):
        pl.semaphore_signal(barrier, inc=1, device_id=device, device_id_type=MESH)

    each(1, groups, lambda o: greet((p, lax.rem(me + o, groups))))
    each(1, n, lambda o: greet((peer(o), me)))
    each(nsub, nsub + 2, lambda i: load_wide(i).start())
    for copy in smalls:
        copy.start()
    each(nsub + 2, early, lambda i: load_wide(i).start())
    each(0, el, lambda e: load_gate(e).start())
    each(0, el, lambda e: load_up(e).start())
    each(early, remote, lambda i: load_wide(i).start())
    each(0, el, lambda e: load_down(e).start())
    each(remote, remote + per_peer, lambda i: load_wide(i).start())
    pl.semaphore_wait(barrier, groups - 1 + n - 1)

    each(nsub, nsub + 2, send_chunk)

    for copy in smalls:
        copy.wait()
    slot = lax.broadcasted_iota(jnp.int32, (total, tok_rows), 0)
    slot_expert = slot // CAP
    chosen = jnp.zeros((total, tok_rows), jnp.float32)
    scale = jnp.zeros((total, tok_rows), jnp.float32)
    for k in range(routes_v.shape[0]):
        hit = routes_v[k : k + 1, :] == slot_expert
        chosen = chosen + jnp.where(hit, 1.0, 0.0)
        scale = scale + jnp.where(hit, weight_v[k : k + 1, :], 0.0)
    row = lax.broadcasted_iota(jnp.int32, (tok_rows, tok_rows), 0)
    col = lax.broadcasted_iota(jnp.int32, (tok_rows, tok_rows), 1)
    before = jnp.where(row < col, 1.0, 0.0).astype(jnp.bfloat16)
    earlier = jnp.dot(chosen.astype(jnp.bfloat16), before, preferred_element_type=jnp.float32)
    placed = (chosen == 1.0) & (earlier == (slot % CAP).astype(jnp.float32))
    combine = jnp.where(placed, scale, 0.0).T
    dispatch = jnp.where(placed, 1.0, 0.0).astype(jnp.bfloat16)
    outgoing[...] = (
        jnp.dot(dispatch, tok_v[...], preferred_element_type=jnp.float32)
        .astype(jnp.bfloat16)
        .reshape(groups, slots, width)
    )
    arrived[me] = outgoing[me]
    spread_all(outgoing, arrived, out_send, out_recv)
    each(nsub + 2, early, send_chunk)

    r = lax.broadcasted_iota(jnp.int32, (total, total), 0)
    c = lax.broadcasted_iota(jnp.int32, (total, total), 1)
    home = ((r // CAP) % groups) * slots + (r // per_expert) * CAP + r % CAP
    order = jnp.where(c == home, 1.0, 0.0)
    gather_all(outgoing, arrived, out_send, out_recv)
    by_expert[...] = (
        jnp.dot(
            order.astype(jnp.bfloat16),
            arrived[...].reshape(total, width),
            preferred_element_type=jnp.float32,
        )
        .astype(jnp.bfloat16)
        .reshape(el, per_expert, width)
    )

    def project(e):
        load_gate(e).wait()
        load_up(e).wait()
        x = by_expert[e]
        at = pl.ds(pl.multiple_of(e * per_expert, 16), per_expert)
        partial[at, :ff] = jnp.dot(x, gate_v[e], preferred_element_type=jnp.float32)
        partial[at, ff:] = jnp.dot(x, up_v[e], preferred_element_type=jnp.float32)

    each(0, el, project)
    to_send[...] = partial[...].reshape(n, share, 2 * ff).astype(jnp.bfloat16)
    each(1, n, lambda o: part_copy(o).start())
    each(early, middle, send_chunk)

    each(1, n, lambda o: part_copy(o).wait_recv())

    def gather_part(o, acc):
        return acc + peers_part[o].astype(jnp.float32)

    summed = lax.fori_loop(1, n, gather_part, partial[share_of(p), :])
    gate, up = summed[:, :ff], summed[:, ff:]
    hidden[share_of(p), :] = (gate / (1.0 + jnp.exp(-gate)) * up).astype(jnp.bfloat16)
    each(1, n, lambda o: hidden_copy(o, p).start())
    each(middle, remote, send_chunk)
    each(1, n, lambda o: hidden_copy(o, lax.rem(p + n - o, n)).wait_recv())

    def contract(e):
        load_down(e).wait()
        h = hidden[pl.ds(pl.multiple_of(e * per_expert, 16), per_expert), :]
        by_expert[e] = jnp.dot(h, down_v[e], preferred_element_type=jnp.float32).astype(
            jnp.bfloat16
        )

    each(0, el, contract)
    leaving[...] = (
        jnp.dot(
            order.T.astype(jnp.bfloat16),
            by_expert[...].reshape(total, width),
            preferred_element_type=jnp.float32,
        )
        .astype(jnp.bfloat16)
        .reshape(groups, slots, width)
    )
    returned[me] = leaving[me]
    spread_all(leaving, returned, ret_send, ret_recv)

    def keep(i):
        load_wide(i).wait()
        _, e, r = chunk_at(i)
        synced[e, pl.ds(pl.multiple_of(p * rows + r, 16), rc), :] = wide[i].astype(jnp.bfloat16)

    each(remote, remote + per_peer, keep)
    gather_all(leaving, returned, ret_send, ret_recv)
    answers = returned[...].reshape(total, width)
    high = combine.astype(jnp.bfloat16)
    rest = combine - high.astype(jnp.float32)
    mid = rest.astype(jnp.bfloat16)
    low = (rest - mid.astype(jnp.float32)).astype(jnp.bfloat16)
    mixed[...] = (
        jnp.dot(low, answers, preferred_element_type=jnp.float32)
        + jnp.dot(mid, answers, preferred_element_type=jnp.float32)
        + jnp.dot(high, answers, preferred_element_type=jnp.float32)
    ).astype(jnp.bfloat16)

    each(
        1, groups,
        lambda o: spread(
            outgoing, arrived, out_send, out_recv, o, lax.rem(me + o, groups)
        ).wait_send(),
    )
    each(
        1, groups,
        lambda o: spread(
            leaving, returned, ret_send, ret_recv, o, lax.rem(me + o, groups)
        ).wait_send(),
    )
    each(1, n, lambda o: part_copy(o).wait_send())
    each(1, n, lambda o: hidden_copy(o, p).wait_send())

    def finish(i):
        sync_copy(i).wait_send()
        sync_arrival(i).wait_recv()

    each(nsub, remote, finish)


def settle(n, mixed, synced, ahead, mixed_out, synced_out, sems):
    p = lax.axis_index("dp")
    rows = ahead.shape[0]
    copies = [pltpu.make_async_copy(mixed, mixed_out, sems.at[0])]
    for o in range(n):
        part = pl.ds(pl.multiple_of(lax.rem(p + o, n) * rows, 16), rows)
        source = ahead if o == n - 1 else synced.at[0, part]
        copies.append(pltpu.make_async_copy(source, synced_out.at[0, part], sems.at[1 + o]))
    for e in range(1, synced.shape[0]):
        copies.append(pltpu.make_async_copy(synced.at[e], synced_out.at[e], sems.at[n + e]))
    for copy in copies:
        copy.start()
    for copy in copies:
        copy.wait()


def local(tokens, routes, route_weight, gate_weight, up_weight, down_weight, trained_down):
    n, groups = lax.axis_size("dp"), lax.axis_size("expert")
    tok_rows, width = tokens.shape
    el, _, ff = gate_weight.shape
    rows = trained_down.shape[1]
    slots = el * CAP
    total = groups * slots
    share = total // n
    fits = [
        d for d in range(16, rows + 1, 16) if rows % d == 0 and d * width * 2 <= CHUNK_BYTES
    ]
    rc = fits[-1]
    nsub = rows // rc
    chunks = n * el * nsub
    bf16, f32 = jnp.bfloat16, jnp.float32
    inside = pl.BlockSpec(memory_space=pltpu.VMEM)
    anywhere = pl.BlockSpec(memory_space=pl.ANY)
    dma = pltpu.SemaphoreType.DMA
    routes, route_weight = routes.T, route_weight.T
    column = lax.rem(lax.axis_index("dp") + 1, n) * width
    block = lax.dynamic_slice(trained_down, (0, 0, column), (1, rows, width))[0]
    ahead = lax.ppermute(block.astype(bf16), "dp", [(i, (i + 1) % n) for i in range(n)])
    results = pl.pallas_call(
        functools.partial(fused, (n, groups, el, rc, nsub)),
        out_shape=(
            pltpu.VMEM((tok_rows, width), bf16),
            pltpu.VMEM((el, n * rows, width), bf16),
        ),
        in_specs=[anywhere] * 7,
        out_specs=(inside, inside),
        scratch_shapes=[
            pltpu.VMEM(tokens.shape, bf16),
            pltpu.VMEM(routes.shape, jnp.int32),
            pltpu.VMEM(route_weight.shape, f32),
            pltpu.VMEM(gate_weight.shape, bf16),
            pltpu.VMEM(up_weight.shape, bf16),
            pltpu.VMEM(down_weight.shape, bf16),
            pltpu.VMEM((chunks, rc, width), f32),
            pltpu.VMEM((chunks - el * nsub, rc, width), bf16),
            pltpu.VMEM((groups, slots, width), bf16),
            pltpu.VMEM((groups, slots, width), bf16),
            pltpu.VMEM((el, total // el, width), bf16),
            pltpu.VMEM((total, 2 * ff), f32),
            pltpu.VMEM((n, share, 2 * ff), bf16),
            pltpu.VMEM((n, share, 2 * ff), bf16),
            pltpu.VMEM((total, ff), bf16),
            pltpu.VMEM((groups, slots, width), bf16),
            pltpu.VMEM((groups, slots, width), bf16),
            dma((3,)),
            dma((3 * el,)),
            dma((chunks,)),
            dma((chunks,)),
            dma((chunks,)),
            dma((groups,)),
            dma((groups,)),
            dma((n,)),
            dma((n,)),
            dma((n,)),
            dma((n,)),
            dma((groups,)),
            dma((groups,)),
        ],
        compiler_params=pltpu.CompilerParams(
            collective_id=0, has_side_effects=True, vmem_limit_bytes=52 * 2**20
        ),
        cost_estimate=pl.CostEstimate(
            flops=6 * total * width * ff, bytes_accessed=2**28, transcendentals=0
        ),
    )(tokens, routes, route_weight, gate_weight, up_weight, down_weight, trained_down)
    return pl.pallas_call(
        functools.partial(settle, n),
        out_shape=(
            jax.ShapeDtypeStruct((tok_rows, width), bf16),
            jax.ShapeDtypeStruct((el, n * rows, width), bf16),
        ),
        in_specs=[inside] * 3,
        out_specs=(anywhere, anywhere),
        scratch_shapes=[dma((n + el,))],
        compiler_params=pltpu.CompilerParams(vmem_limit_bytes=2**20),
    )(*(pltpu.with_memory_space_constraint(x, pltpu.VMEM) for x in (*results, ahead)))


def solution(mesh):
    placed = (
        P("expert", "dp"),
        P("expert", None),
        P("expert", None),
        P("expert", "dp", None),
        P("expert", "dp", None),
        P("expert", None, "dp"),
        P("expert", "dp", None),
    )
    return jax.shard_map(
        local,
        mesh=mesh,
        in_specs=placed,
        out_specs=(P("expert", "dp"), P("expert", None, "dp")),
        check_vma=False,
    )
```

profile of v0, /device:TPU:1, one launch (start us, length us, event | category | flops | bytes accessed | tf_op | source)
XLA Modules:
  0.0 89.1 jit_solution(2706989698767957052)
XLA Ops:
  0.6 1.5 %fusion = bf16[384,1024]{1,0:T(8,128)(2,1)S(1)} fusion(f32[4,384,2048]{2,1,0:T(8,128)} %trained.1, s32[]{:T(128)S(6)} %select_n.3), kind=kLoop, calls=%fused_computation.1 | loop fusion | bytes 1572868 | tf_op jit(solution)/shard_map/convert_element_type | solution.py:341
  2.2 2.1 %collective-permute-start = (bf16[384,1024]{1,0:T(8,128)(2,1)S(1)}, bf16[384,1024]{1,0:T(8,128)(2,1)S(1)}, u32[]{:S(2)}, u32[]{:S(2)}) collective-permute-start(bf16[384,1024]{1,0:T(8,128)(2,1)S(1)} %fusion), channel_id=1, source_target_pairs={{0,16},{16,0},{1,17},{17,1},{2,18},{18,2},{3,19},{19,3},{4,20},{20... | collective-permute-start | bytes 2359304 | tf_op jit(solution)/shard_map/ppermute | solution.py:341
  4.3 82.1 %shard_map.86 = (bf16[32,1024]{1,0:T(8,128)(2,1)S(1)}, bf16[4,768,1024]{2,1,0:T(8,128)(2,1)S(1)}) custom-call(bf16[32,1024]{1,0:T(8,128)(2,1)} %tokens.1, s32[8,32]{1,0:T(8,128)} %bitcast.4, f32[8,32]{1,0:T(8,128)} %bitcast.5, bf16[4,1024,768]{2,1,0:T(8,128)(2,1)} %gate_weight.1, bf16[4,1024,768]{2,1,0:T(8,128)(2,1)} %up_weight.1, ...), custom_call_target="tpu_custom_call" | custom-call | flops 1207959552 | bytes 268435456 | tf_op jit(solution)/shard_map/pallas_call | solution.py:342
  86.4 0.0 collective-permute-done.ahead
  86.4 2.8 %shard_map.87 = (bf16[32,1024]{1,0:T(8,128)(2,1)}, bf16[4,768,1024]{2,1,0:T(8,128)(2,1)}) custom-call(bf16[32,1024]{1,0:T(8,128)(2,1)S(1)} %get-tuple-element.4.mixed, bf16[4,768,1024]{2,1,0:T(8,128)(2,1)S(1)} %get-tuple-element.5.synced, bf16[384,1024]{1,0:T(8,128)(2,1)S(1)} %collective-permute-done.ahead), custom_call_target="tpu_custom_call" | custom-call | tf_op jit(solution)/shard_map/pallas_call | solution.py:389
Async XLA Ops:
  2.2 84.2 %collective-permute-start = (bf16[384,1024]{1,0:T(8,128)(2,1)S(1)}, bf16[384,1024]{1,0:T(8,128)(2,1)S(1)}, u32[]{:S(2)}, u32[]{:S(2)}) collective-permute-start(bf16[384,1024]{1,0:T(8,128)(2,1)S(1)} %fusion), channel_id=1, source_target_pairs={{0,16},{16,0},{1,17},{17,1},{2,18},{18,2},{3,19},{19,3},{4,20},{20... | collective-permute-start | bytes 2359304 | tf_op jit(solution)/shard_map/ppermute | solution.py:341
where the time goes:
time: 90.5 us; the launch traced here: 89.1 us
  Pallas kernels  84.9 us (94%)
  starting transfers between devices  2.09 us (2%)
  local copies, waits for them, and re-layouts  1.53 us (2%)
    pallas_call x1, Pallas kernels, local(): pl.pallas_call(functools.partial(fused, (n, groups, el, rc, nsub)), out_s...  82.1 us
    pallas_call x1, Pallas kernels, local(): pl.pallas_call(functools.partial(settle, n), out_shape=(jax.ShapeDtypeStr...  2.77 us
    ppermute x1, starting transfers between devices, local(): lax.ppermute(block.astype(bf16), 'dp', [(i, (i + 1) % n) for i in range(n)])  2.09 us
  transfers between devices with their start and end apart: 1, of which 0 were waited for; matrix products, arithmetic and copies ran while one was open for 0% of the time, Pallas kernels for 92%

commit v1 on v0

--- a/solution.py
+++ b/solution.py
@@ -9,9 +9,30 @@
 
 CAP = 4
 CHUNK_BYTES = 200_000
-EARLY = 1 / 4
-MIDDLE = 3 / 16
+FIRST = 2
+EARLY = 5 / 16
+MIDDLE = 1 / 16
+LATE = 1 / 4
 MESH = pl.DeviceIdType.MESH
+
+
+def each(start, stop, body):
+    def step(i, carry):
+        body(i)
+        return carry
+
+    lax.fori_loop(start, stop, step, 0)
+
+
+def chunk_at(dims, i):
+    n, _, el, rc, nsub, _ = dims
+    offset = lax.rem(lax.div(i, el * nsub) + 1, n)
+    e = lax.rem(lax.div(i, nsub), el)
+    return offset, e, lax.rem(i, nsub) * rc
+
+
+def rows_of(dims, rows, source, r):
+    return pl.ds(pl.multiple_of(source * rows + r, 16), dims[3])
 
 
 def fused(
@@ -23,9 +44,11 @@
     leaving, returned,
     small_sem, load_sem, wide_sem, sync_send, sync_recv,
     out_send, out_recv, part_send, part_recv, hid_send, hid_recv, ret_send, ret_recv,
+    entered,
 ):
-    n, groups, el, rc, nsub = dims
+    n, groups, el, rc, nsub, late = dims
     p, me = lax.axis_index("dp"), lax.axis_index("expert")
+    core = lax.rem(me, 2)
     rows = trained.shape[1]
     tok_rows, width = tok_v.shape
     ff = gate_v.shape[2]
@@ -35,8 +58,9 @@
     per_expert = total // el
     per_peer = el * nsub
     remote = (n - 1) * per_peer
-    early = nsub + round(remote * EARLY)
+    early = round(remote * EARLY)
     middle = early + round(remote * MIDDLE)
+    own = remote - core * late
 
     def peer(offset):
         return lax.rem(p + offset, n)
@@ -44,23 +68,18 @@
     def share_of(device):
         return pl.ds(pl.multiple_of(device * share, 16), share)
 
-    def chunk_at(i):
-        offset = lax.rem(lax.div(i, per_peer) + 1, n)
-        e = lax.rem(lax.div(i, nsub), el)
-        return offset, e, lax.rem(i, nsub) * rc
-
     def load_wide(i):
-        offset, e, r = chunk_at(i)
+        offset, e, r = chunk_at(dims, i)
         cols = pl.ds(pl.multiple_of(peer(offset) * width, 128), width)
         return pltpu.make_async_copy(
             trained.at[e, pl.ds(pl.multiple_of(r, 16), rc), cols], wide.at[i], wide_sem.at[i]
         )
 
     def sync_copy(i):
-        offset, e, r = chunk_at(i)
+        offset, e, r = chunk_at(dims, i)
         return pltpu.make_async_remote_copy(
             src_ref=narrow.at[i],
-            dst_ref=synced.at[e, pl.ds(pl.multiple_of(p * rows + r, 16), rc), :],
+            dst_ref=synced.at[e, rows_of(dims, rows, p, r), :],
             send_sem=sync_send.at[i],
             recv_sem=sync_recv.at[i],
             device_id=(peer(offset), me),
@@ -68,23 +87,16 @@
         )
 
     def sync_arrival(i):
-        offset, e, r = chunk_at(i)
+        offset, e, r = chunk_at(dims, i)
         source = lax.rem(p + n - offset, n)
         return pltpu.make_async_remote_copy(
             src_ref=narrow.at[i],
-            dst_ref=synced.at[e, pl.ds(pl.multiple_of(source * rows + r, 16), rc), :],
+            dst_ref=synced.at[e, rows_of(dims, rows, source, r), :],
             send_sem=sync_send.at[i],
             recv_sem=sync_recv.at[i],
             device_id=(peer(offset), me),
             device_id_type=MESH,
         )
-
-    def each(start, stop, body):
-        def step(i, carry):
-            body(i)
-            return carry
-
-        lax.fori_loop(start, stop, step, 0)
 
     def send_chunk(i):
         load_wide(i).wait()
@@ -160,20 +172,37 @@
     def greet(device):
         pl.semaphore_signal(barrier, inc=1, device_id=device, device_id_type=MESH)
 
-    each(1, groups, lambda o: greet((p, lax.rem(me + o, groups))))
+    leader = me - core
     each(1, n, lambda o: greet((peer(o), me)))
-    each(nsub, nsub + 2, lambda i: load_wide(i).start())
+
+    @pl.when(core == 0)
+    def _():
+        greet((p, me + 1))
+
+    @pl.when(core == 1)
+    def _():
+        each(0, groups // 2, lambda j: greet((p, lax.rem(leader + 2 * j, groups))))
+
+    @pl.when(core == 0)
+    def _():
+        each(1, groups // 2, lambda j: greet((p, lax.rem(leader + 2 * j, groups))))
+
+    each(0, FIRST, lambda i: load_wide(i).start())
     for copy in smalls:
         copy.start()
-    each(nsub + 2, early, lambda i: load_wide(i).start())
+    each(FIRST, early, lambda i: load_wide(i).start())
     each(0, el, lambda e: load_gate(e).start())
     each(0, el, lambda e: load_up(e).start())
-    each(early, remote, lambda i: load_wide(i).start())
+    each(early, own, lambda i: load_wide(i).start())
     each(0, el, lambda e: load_down(e).start())
     each(remote, remote + per_peer, lambda i: load_wide(i).start())
-    pl.semaphore_wait(barrier, groups - 1 + n - 1)
-
-    each(nsub, nsub + 2, send_chunk)
+    pl.semaphore_wait(barrier, n - 1 + jnp.where(core == 0, groups - 1, 1))
+
+    @pl.when(core == 0)
+    def _():
+        pl.semaphore_signal(entered, inc=1, device_id=(p, me + 1), device_id_type=MESH)
+
+    each(0, FIRST, send_chunk)
 
     for copy in smalls:
         copy.wait()
@@ -198,8 +227,13 @@
         .reshape(groups, slots, width)
     )
     arrived[me] = outgoing[me]
+
+    @pl.when(core == 1)
+    def _():
+        pl.semaphore_wait(entered, 1)
+
     spread_all(outgoing, arrived, out_send, out_recv)
-    each(nsub + 2, early, send_chunk)
+    each(FIRST, early, send_chunk)
 
     r = lax.broadcasted_iota(jnp.int32, (total, total), 0)
     c = lax.broadcasted_iota(jnp.int32, (total, total), 1)
@@ -238,7 +272,7 @@
     gate, up = summed[:, :ff], summed[:, ff:]
     hidden[share_of(p), :] = (gate / (1.0 + jnp.exp(-gate)) * up).astype(jnp.bfloat16)
     each(1, n, lambda o: hidden_copy(o, p).start())
-    each(middle, remote, send_chunk)
+    each(middle, own, send_chunk)
     each(1, n, lambda o: hidden_copy(o, lax.rem(p + n - o, n)).wait_recv())
 
     def contract(e):
@@ -263,8 +297,8 @@
 
     def keep(i):
         load_wide(i).wait()
-        _, e, r = chunk_at(i)
-        synced[e, pl.ds(pl.multiple_of(p * rows + r, 16), rc), :] = wide[i].astype(jnp.bfloat16)
+        _, e, r = chunk_at(dims, i)
+        synced[e, rows_of(dims, rows, p, r), :] = wide[i].astype(jnp.bfloat16)
 
     each(remote, remote + per_peer, keep)
     gather_all(leaving, returned, ret_send, ret_recv)
@@ -298,23 +332,92 @@
         sync_copy(i).wait_send()
         sync_arrival(i).wait_recv()
 
-    each(nsub, remote, finish)
-
-
-def settle(n, mixed, synced, ahead, mixed_out, synced_out, sems):
-    p = lax.axis_index("dp")
-    rows = ahead.shape[0]
-    copies = [pltpu.make_async_copy(mixed, mixed_out, sems.at[0])]
-    for o in range(n):
-        part = pl.ds(pl.multiple_of(lax.rem(p + o, n) * rows, 16), rows)
-        source = ahead if o == n - 1 else synced.at[0, part]
-        copies.append(pltpu.make_async_copy(source, synced_out.at[0, part], sems.at[1 + o]))
-    for e in range(1, synced.shape[0]):
-        copies.append(pltpu.make_async_copy(synced.at[e], synced_out.at[e], sems.at[n + e]))
-    for copy in copies:
-        copy.start()
-    for copy in copies:
-        copy.wait()
+    each(0, own, finish)
+
+
+def store(dims, mixed, synced, mixed_out, synced_out, mark, sems):
+    n, _, el, _, nsub, late = dims
+    p, core = lax.axis_index("dp"), lax.rem(lax.axis_index("expert"), 2)
+    rows = synced.shape[1] // n
+    own = (n - 1) * el * nsub - core * late
+
+    def local_part(e):
+        part = pl.ds(pl.multiple_of(p * rows, 16), rows)
+        return pltpu.make_async_copy(synced.at[e, part], synced_out.at[e, part], sems.at[e])
+
+    def arrived_part(i):
+        offset, e, r = chunk_at(dims, i)
+        part = rows_of(dims, rows, lax.rem(p + n - offset, n), r)
+        return pltpu.make_async_copy(synced.at[e, part], synced_out.at[e, part], sems.at[el + i])
+
+    out = pltpu.make_async_copy(mixed, mixed_out, sems.at[sems.shape[0] - 1])
+    each(0, el, lambda e: local_part(e).start())
+    each(0, own, lambda i: arrived_part(i).start())
+    out.start()
+    mark[...] = jnp.zeros_like(mark)
+    each(0, el, lambda e: local_part(e).wait())
+    each(0, own, lambda i: arrived_part(i).wait())
+    out.wait()
+
+
+def trailing(dims, trained, mark, tail, wide, narrow, wide_sem, send_sem, recv_sem):
+    n, _, el, rc, nsub, late = dims
+    p, me = lax.axis_index("dp"), lax.axis_index("expert")
+    width = wide.shape[2]
+    first = (n - 1) * el * nsub - late
+    stop = lax.rem(me, 2) * late
+
+    def load(i):
+        offset, e, r = chunk_at(dims, first + i)
+        cols = pl.ds(pl.multiple_of(lax.rem(p + offset, n) * width, 128), width)
+        return pltpu.make_async_copy(
+            trained.at[e, pl.ds(pl.multiple_of(r, 16), rc), cols], wide.at[i], wide_sem.at[i]
+        )
+
+    def copy(i):
+        offset, _, _ = chunk_at(dims, first + i)
+        return pltpu.make_async_remote_copy(
+            src_ref=narrow.at[i],
+            dst_ref=tail.at[i],
+            send_sem=send_sem.at[i],
+            recv_sem=recv_sem.at[i],
+            device_id=(lax.rem(p + offset, n), me),
+            device_id_type=MESH,
+        )
+
+    def send(i):
+        load(i).wait()
+        narrow[i] = wide[i].astype(jnp.bfloat16)
+        copy(i).start()
+
+    barrier = pltpu.get_barrier_semaphore()
+    each(
+        1, n,
+        lambda o: pl.semaphore_signal(
+            barrier, inc=1, device_id=(lax.rem(p + o, n), me), device_id_type=MESH
+        ),
+    )
+    each(0, stop, lambda i: load(i).start())
+    pl.semaphore_wait(barrier, n - 1)
+    each(0, stop, send)
+    each(0, stop, lambda i: copy(i).wait())
+
+
+def settle(dims, tail, stored, synced_out, sems):
+    n, _, el, _, nsub, late = dims
+    p, core = lax.axis_index("dp"), lax.rem(lax.axis_index("expert"), 2)
+    rows = synced_out.shape[1] // n
+    first = (n - 1) * el * nsub - late
+
+    def part(i):
+        offset, e, r = chunk_at(dims, first + i)
+        source = lax.rem(p + n - offset, n)
+        return pltpu.make_async_copy(
+            tail.at[i], synced_out.at[e, rows_of(dims, rows, source, r)], sems.at[i]
+        )
+
+    each(0, core * late, lambda i: part(i).start())
+    each(0, core * late, lambda i: part(i).wait())
 
 
 def local(tokens, routes, route_weight, gate_weight, up_weight, down_weight, trained_down):
@@ -331,16 +434,20 @@
     rc = fits[-1]
     nsub = rows // rc
     chunks = n * el * nsub
+    remote = chunks - el * nsub
+    late = round(remote * LATE)
+    dims = (n, groups, el, rc, nsub, late)
     bf16, f32 = jnp.bfloat16, jnp.float32
     inside = pl.BlockSpec(memory_space=pltpu.VMEM)
     anywhere = pl.BlockSpec(memory_space=pl.ANY)
     dma = pltpu.SemaphoreType.DMA
     routes, route_weight = routes.T, route_weight.T
-    column = lax.rem(lax.axis_index("dp") + 1, n) * width
-    block = lax.dynamic_slice(trained_down, (0, 0, column), (1, rows, width))[0]
-    ahead = lax.ppermute(block.astype(bf16), "dp", [(i, (i + 1) % n) for i in range(n)])
-    results = pl.pallas_call(
-        functools.partial(fused, (n, groups, el, rc, nsub)),
+
+    def in_vmem(x):
+        return pltpu.with_memory_space_constraint(x, pltpu.VMEM)
+
+    mixed, synced = pl.pallas_call(
+        functools.partial(fused, dims),
         out_shape=(
             pltpu.VMEM((tok_rows, width), bf16),
             pltpu.VMEM((el, n * rows, width), bf16),
@@ -355,7 +462,7 @@
             pltpu.VMEM(up_weight.shape, bf16),
             pltpu.VMEM(down_weight.shape, bf16),
             pltpu.VMEM((chunks, rc, width), f32),
-            pltpu.VMEM((chunks - el * nsub, rc, width), bf16),
+            pltpu.VMEM((remote, rc, width), bf16),
             pltpu.VMEM((groups, slots, width), bf16),
             pltpu.VMEM((groups, slots, width), bf16),
             pltpu.VMEM((el, total // el, width), bf16),
@@ -368,8 +475,8 @@
             dma((3,)),
             dma((3 * el,)),
             dma((chunks,)),
-            dma((chunks,)),
-            dma((chunks,)),
+            dma((remote,)),
+            dma((remote,)),
             dma((groups,)),
             dma((groups,)),
             dma((n,)),
@@ -378,6 +485,7 @@
             dma((n,)),
             dma((groups,)),
             dma((groups,)),
+            pltpu.SemaphoreType.REGULAR,
         ],
         compiler_params=pltpu.CompilerParams(
             collective_id=0, has_side_effects=True, vmem_limit_bytes=52 * 2**20
@@ -386,17 +494,44 @@
             flops=6 * total * width * ff, bytes_accessed=2**28, transcendentals=0
         ),
     )(tokens, routes, route_weight, gate_weight, up_weight, down_weight, trained_down)
-    return pl.pallas_call(
-        functools.partial(settle, n),
+    mixed, stored, mark = pl.pallas_call(
+        functools.partial(store, dims),
         out_shape=(
             jax.ShapeDtypeStruct((tok_rows, width), bf16),
             jax.ShapeDtypeStruct((el, n * rows, width), bf16),
+            pltpu.VMEM((8, 128), f32),
         ),
-        in_specs=[inside] * 3,
-        out_specs=(anywhere, anywhere),
-        scratch_shapes=[dma((n + el,))],
+        in_specs=[inside] * 2,
+        out_specs=(anywhere, anywhere, inside),
+        scratch_shapes=[dma((el + remote + 1,))],
         compiler_params=pltpu.CompilerParams(vmem_limit_bytes=2**20),
-    )(*(pltpu.with_memory_space_constraint(x, pltpu.VMEM) for x in (*results, ahead)))
+    )(in_vmem(mixed), in_vmem(synced))
+    tail = pl.pallas_call(
+        functools.partial(trailing, dims),
+        out_shape=pltpu.VMEM((late, rc, width), bf16),
+        in_specs=[anywhere] * 2,
+        out_specs=inside,
+        scratch_shapes=[
+            pltpu.VMEM((late, rc, width), f32),
+            pltpu.VMEM((late, rc, width), bf16),
+            dma((late,)),
+            dma((late,)),
+            dma((late,)),
+        ],
+        compiler_params=pltpu.CompilerParams(
+            collective_id=1, has_side_effects=True, vmem_limit_bytes=56 * 2**20
+        ),
+    )(trained_down, in_vmem(mark))
+    synced = pl.pallas_call(
+        functools.partial(settle, dims),
+        out_shape=jax.ShapeDtypeStruct((el, n * rows, width), bf16),
+        in_specs=[inside, anywhere],
+        out_specs=anywhere,
+        scratch_shapes=[dma((late,))],
+        input_output_aliases={1: 0},
+        compiler_params=pltpu.CompilerParams(vmem_limit_bytes=2**20),
+    )(in_vmem(tail), stored)
+    return mixed, synced
 
 
 def solution(mesh):

time: 90.5 us -> 87.7 us (0.969)
  the two profiles are of different devices: /device:TPU:1 before, /device:TPU:0 now
where the time goes in v1:
time: 87.7 us; the launch traced here: 87.5 us
  Pallas kernels  86.9 us (99%)
    pallas_call x1, Pallas kernels, local(): pl.pallas_call(functools.partial(fused, dims), out_shape=(pltpu.VMEM((tok...  83.8 us
    pallas_call x1, Pallas kernels, local(): pl.pallas_call(functools.partial(store, dims), out_shape=(jax.ShapeDtypeS...  2.84 us

profile of v1, /device:TPU:0, one launch (start us, length us, event | category | flops | bytes accessed | tf_op | source)
XLA Modules:
  0.0 87.5 jit_solution(16466936687770350897)
XLA Ops:
  0.6 83.8 %shard_map.86 = (bf16[32,1024]{1,0:T(8,128)(2,1)S(1)}, bf16[4,768,1024]{2,1,0:T(8,128)(2,1)S(1)}) custom-call(bf16[32,1024]{1,0:T(8,128)(2,1)} %tokens.1, s32[8,32]{1,0:T(8,128)} %bitcast.2, f32[8,32]{1,0:T(8,128)} %bitcast.3, bf16[4,1024,768]{2,1,0:T(8,128)(2,1)} %gate_weight.1, bf16[4,1024,768]{2,1,0:T(8,128)(2,1)} %up_weight.1, ...), custom_call_target="tpu_custom_call" | custom-call | flops 1207959552 | bytes 268435456 | tf_op jit(solution)/shard_map/pallas_call | solution.py:449
  84.4 2.8 %shard_map.87 = (bf16[32,1024]{1,0:T(8,128)(2,1)}, bf16[4,768,1024]{2,1,0:T(8,128)(2,1)}, f32[8,128]{1,0:T(8,128)S(1)}) custom-call(bf16[32,1024]{1,0:T(8,128)(2,1)S(1)} %get-tuple-element.7.mixed, bf16[4,768,1024]{2,1,0:T(8,128)(2,1)S(1)} %get-tuple-element.8.synced), custom_call_target="tpu_custom_call" | custom-call | tf_op jit(solution)/shard_map/pallas_call | solution.py:497
  87.3 0.2 shard_map.88.tail
  87.5 0.1 shard_map.89

commit v2 on v1

--- a/solution.py
+++ b/solution.py
@@ -12,7 +12,8 @@
 FIRST = 2
 EARLY = 5 / 16
 MIDDLE = 1 / 16
-LATE = 1 / 4
+LATE = 3 / 16
+COVER = 4
 MESH = pl.DeviceIdType.MESH
 
 
@@ -44,7 +45,7 @@
     leaving, returned,
     small_sem, load_sem, wide_sem, sync_send, sync_recv,
     out_send, out_recv, part_send, part_recv, hid_send, hid_recv, ret_send, ret_recv,
-    entered,
+    entered, nearly,
 ):
     n, groups, el, rc, nsub, late = dims
     p, me = lax.axis_index("dp"), lax.axis_index("expert")
@@ -172,6 +173,7 @@
     def greet(device):
         pl.semaphore_signal(barrier, inc=1, device_id=device, device_id_type=MESH)
 
+    each(0, FIRST, lambda i: load_wide(i).start())
     leader = me - core
     each(1, n, lambda o: greet((peer(o), me)))
 
@@ -187,7 +189,6 @@
     def _():
         each(1, groups // 2, lambda j: greet((p, lax.rem(leader + 2 * j, groups))))
 
-    each(0, FIRST, lambda i: load_wide(i).start())
     for copy in smalls:
         copy.start()
     each(FIRST, early, lambda i: load_wide(i).start())
@@ -332,7 +333,17 @@
         sync_copy(i).wait_send()
         sync_arrival(i).wait_recv()
 
-    each(0, own, finish)
+    each(0, own - COVER, finish)
+
+    @pl.when(core == 0)
+    def _():
+        pl.semaphore_signal(nearly, inc=1, device_id=(p, me + 1), device_id_type=MESH)
+
+    each(own - COVER, own, finish)
+
+    @pl.when(core == 1)
+    def _():
+        pl.semaphore_wait(nearly, 1)
 
 
 def store(dims, mixed, synced, mixed_out, synced_out, mark, sems):
@@ -485,6 +496,7 @@
             dma((n,)),
             dma((groups,)),
             dma((groups,)),
+            pltpu.SemaphoreType.REGULAR,
             pltpu.SemaphoreType.REGULAR,
         ],
         compiler_params=pltpu.CompilerParams(

time: 87.7 us -> 85.9 us (0.979)
  the two profiles are of different devices: /device:TPU:0 before, /device:TPU:1 now
where the time goes in v2:
time: 85.9 us; the launch traced here: 85.8 us
  Pallas kernels  85.1 us (99%)
    pallas_call x1, Pallas kernels, local(): pl.pallas_call(functools.partial(fused, dims), out_shape=(pltpu.VMEM((tok...  71.5 us
    pallas_call x1, Pallas kernels, local(): pl.pallas_call(functools.partial(trailing, dims), out_shape=pltpu.VMEM((l...  10.1 us
    pallas_call x1, Pallas kernels, local(): pl.pallas_call(functools.partial(store, dims), out_shape=(jax.ShapeDtypeS...  2.67 us

profile of v2, /device:TPU:1, one launch (start us, length us, event | category | flops | bytes accessed | tf_op | source)
XLA Modules:
  0.0 85.8 jit_solution(7368123570092438904)
XLA Ops:
  0.6 71.5 %shard_map.86 = (bf16[32,1024]{1,0:T(8,128)(2,1)S(1)}, bf16[4,768,1024]{2,1,0:T(8,128)(2,1)S(1)}) custom-call(bf16[32,1024]{1,0:T(8,128)(2,1)} %tokens.1, s32[8,32]{1,0:T(8,128)} %bitcast.2, f32[8,32]{1,0:T(8,128)} %bitcast.3, bf16[4,1024,768]{2,1,0:T(8,128)(2,1)} %gate_weight.1, bf16[4,1024,768]{2,1,0:T(8,128)(2,1)} %up_weight.1, ...), custom_call_target="tpu_custom_call" | custom-call | flops 1207959552 | bytes 268435456 | tf_op jit(solution)/shard_map/pallas_call | solution.py:460
  72.1 2.7 %shard_map.87 = (bf16[32,1024]{1,0:T(8,128)(2,1)}, bf16[4,768,1024]{2,1,0:T(8,128)(2,1)}, f32[8,128]{1,0:T(8,128)S(1)}) custom-call(bf16[32,1024]{1,0:T(8,128)(2,1)S(1)} %get-tuple-element.7.mixed, bf16[4,768,1024]{2,1,0:T(8,128)(2,1)S(1)} %get-tuple-element.8.synced), custom_call_target="tpu_custom_call" | custom-call | tf_op jit(solution)/shard_map/pallas_call | solution.py:509
  74.8 10.1 %shard_map.88.tail = bf16[3,96,1024]{2,1,0:T(8,128)(2,1)S(1)} custom-call(f32[4,384,2048]{2,1,0:T(8,128)} %trained.3, f32[8,128]{1,0:T(8,128)S(1)} %get-tuple-element.10.mark), custom_call_target="tpu_custom_call" | custom-call | tf_op jit(solution)/shard_map/pallas_call | solution.py:521
  84.9 0.9 %shard_map.89 = bf16[4,768,1024]{2,1,0:T(8,128)(2,1)} custom-call(bf16[3,96,1024]{2,1,0:T(8,128)(2,1)S(1)} %shard_map.88.tail, bf16[4,768,1024]{2,1,0:T(8,128)(2,1)} %get-tuple-element.11.stored), custom_call_target="tpu_custom_call", output_to_operand_aliasing={{}: (1, {})} | custom-call | tf_op jit(solution)/shard_map/pallas_call | solution.py:537

commit v3 on v2

--- a/solution.py
+++ b/solution.py
@@ -14,6 +14,7 @@
 MIDDLE = 1 / 16
 LATE = 3 / 16
 COVER = 4
+TILT = 8
 MESH = pl.DeviceIdType.MESH
 
 
@@ -32,6 +33,10 @@
     return offset, e, lax.rem(i, nsub) * rc
 
 
+def tilt_of(n, total):
+    return total // TILT // 16 * 16 if n == 2 else 0
+
+
 def rows_of(dims, rows, source, r):
     return pl.ds(pl.multiple_of(source * rows + r, 16), dims[3])
 
@@ -40,12 +45,12 @@
     dims,
     tokens, routes, route_weight, gate_weight, up_weight, down_weight, trained,
     mixed, synced,
-    tok_v, routes_v, weight_v, gate_v, up_v, down_v, wide, narrow,
-    outgoing, arrived, by_expert, partial, to_send, peers_part, hidden,
+    tok_v, routes_v, weight_v, gate_v, up_v, down_v, wide, kept, narrow,
+    outgoing, arrived, by_expert, partial, to_send, peers_part, to_tilt, peers_tilt, hidden,
     leaving, returned,
-    small_sem, load_sem, wide_sem, sync_send, sync_recv,
+    small_sem, load_sem, wide_sem, kept_sem, sync_send, sync_recv,
     out_send, out_recv, part_send, part_recv, hid_send, hid_recv, ret_send, ret_recv,
-    entered, nearly,
+    tilt_sem, entered, nearly,
 ):
     n, groups, el, rc, nsub, late = dims
     p, me = lax.axis_index("dp"), lax.axis_index("expert")
@@ -55,7 +60,9 @@
     ff = gate_v.shape[2]
     slots = el * CAP
     total = groups * slots
-    share = total // n
+    tilt = tilt_of(n, total)
+    share = (total - tilt) // n
+    tilted = pl.ds(n * share, tilt)
     per_expert = total // el
     per_peer = el * nsub
     remote = (n - 1) * per_peer
@@ -99,17 +106,21 @@
             device_id_type=MESH,
         )
 
+    load_kept = pltpu.make_async_copy(
+        trained.at[:, :, pl.ds(pl.multiple_of(p * width, 128), width)], kept, kept_sem
+    )
+
     def send_chunk(i):
         load_wide(i).wait()
         narrow[i] = wide[i].astype(jnp.bfloat16)
         sync_copy(i).start()
 
-    def spread(source, target, send, recv, offset, slot):
+    def spread(source, target, send, recv, slot):
         return pltpu.make_async_remote_copy(
             src_ref=source.at[slot],
             dst_ref=target.at[me],
-            send_sem=send.at[offset],
-            recv_sem=recv.at[offset],
+            send_sem=send,
+            recv_sem=recv,
             device_id=(p, slot),
             device_id_type=MESH,
         )
@@ -117,22 +128,19 @@
     def spread_all(source, target, send, recv):
         each(
             1, groups,
-            lambda o: spread(source, target, send, recv, o, lax.rem(me + o, groups)).start(),
-        )
-
-    def gather_all(source, target, send, recv):
-        def body(o):
-            origin = lax.rem(me + groups - o, groups)
-            pltpu.make_async_remote_copy(
-                src_ref=source.at[origin],
-                dst_ref=target.at[origin],
-                send_sem=send.at[o],
-                recv_sem=recv.at[o],
-                device_id=(p, origin),
-                device_id_type=MESH,
-            ).wait_recv()
-
-        each(1, groups, body)
+            lambda o: spread(source, target, send, recv, lax.rem(me + o, groups)).start(),
+        )
+
+    def blocks(source, target, send, recv):
+        some = pl.ds(0, groups - 1)
+        return pltpu.make_async_remote_copy(
+            src_ref=source.at[some],
+            dst_ref=target.at[some],
+            send_sem=send,
+            recv_sem=recv,
+            device_id=(p, lax.rem(me + 1, groups)),
+            device_id_type=MESH,
+        )
 
     def part_copy(o):
         return pltpu.make_async_remote_copy(
@@ -153,6 +161,24 @@
             device_id=(peer(o), me),
             device_id_type=MESH,
         )
+
+    def tilt_copy(source, target, k, device):
+        return pltpu.make_async_remote_copy(
+            src_ref=source,
+            dst_ref=target,
+            send_sem=tilt_sem.at[k],
+            recv_sem=tilt_sem.at[k + 1],
+            device_id=(device, me),
+            device_id_type=MESH,
+        )
+
+    if tilt:
+        tilt_part = tilt_copy(to_tilt, peers_tilt, 0, 1)
+        tilt_hidden = tilt_copy(hidden.at[tilted, :], hidden.at[tilted, :], 2, 0)
+
+    def activate(summed):
+        gate, up = summed[:, :ff], summed[:, ff:]
+        return (gate / (1.0 + jnp.exp(-gate)) * up).astype(jnp.bfloat16)
 
     smalls = [
         pltpu.make_async_copy(src, dst, small_sem.at[i])
@@ -196,7 +222,7 @@
     each(0, el, lambda e: load_up(e).start())
     each(early, own, lambda i: load_wide(i).start())
     each(0, el, lambda e: load_down(e).start())
-    each(remote, remote + per_peer, lambda i: load_wide(i).start())
+    load_kept.start()
     pl.semaphore_wait(barrier, n - 1 + jnp.where(core == 0, groups - 1, 1))
 
     @pl.when(core == 0)
@@ -240,7 +266,7 @@
     c = lax.broadcasted_iota(jnp.int32, (total, total), 1)
     home = ((r // CAP) % groups) * slots + (r // per_expert) * CAP + r % CAP
     order = jnp.where(c == home, 1.0, 0.0)
-    gather_all(outgoing, arrived, out_send, out_recv)
+    blocks(outgoing, arrived, out_send, out_recv).wait_recv()
     by_expert[...] = (
         jnp.dot(
             order.astype(jnp.bfloat16),
@@ -260,8 +286,15 @@
         partial[at, ff:] = jnp.dot(x, up_v[e], preferred_element_type=jnp.float32)
 
     each(0, el, project)
-    to_send[...] = partial[...].reshape(n, share, 2 * ff).astype(jnp.bfloat16)
+    to_send[...] = partial[: n * share].reshape(n, share, 2 * ff).astype(jnp.bfloat16)
     each(1, n, lambda o: part_copy(o).start())
+    if tilt:
+        to_tilt[...] = partial[n * share :].astype(jnp.bfloat16)
+
+        @pl.when(p == 0)
+        def _():
+            tilt_part.start()
+
     each(early, middle, send_chunk)
 
     each(1, n, lambda o: part_copy(o).wait_recv())
@@ -270,11 +303,24 @@
         return acc + peers_part[o].astype(jnp.float32)
 
     summed = lax.fori_loop(1, n, gather_part, partial[share_of(p), :])
-    gate, up = summed[:, :ff], summed[:, ff:]
-    hidden[share_of(p), :] = (gate / (1.0 + jnp.exp(-gate)) * up).astype(jnp.bfloat16)
+    hidden[share_of(p), :] = activate(summed)
     each(1, n, lambda o: hidden_copy(o, p).start())
+    if tilt:
+
+        @pl.when(p == 1)
+        def _():
+            tilt_part.wait_recv()
+            hidden[tilted, :] = activate(partial[tilted, :] + peers_tilt[...].astype(jnp.float32))
+            tilt_hidden.start()
+
     each(middle, own, send_chunk)
     each(1, n, lambda o: hidden_copy(o, lax.rem(p + n - o, n)).wait_recv())
+    if tilt:
+
+        @pl.when(p == 0)
+        def _():
+            tilt_hidden.wait_recv()
+
 
     def contract(e):
         load_down(e).wait()
@@ -296,13 +342,13 @@
     returned[me] = leaving[me]
     spread_all(leaving, returned, ret_send, ret_recv)
 
-    def keep(i):
-        load_wide(i).wait()
-        _, e, r = chunk_at(dims, i)
-        synced[e, rows_of(dims, rows, p, r), :] = wide[i].astype(jnp.bfloat16)
-
-    each(remote, remote + per_peer, keep)
-    gather_all(leaving, returned, ret_send, ret_recv)
+    load_kept.wait()
+
+    def keep(e):
+        synced[e, pl.ds(pl.multiple_of(p * rows, 16), rows), :] = kept[e].astype(jnp.bfloat16)
+
+    each(0, el, keep)
+    blocks(leaving, returned, ret_send, ret_recv).wait_recv()
     answers = returned[...].reshape(total, width)
     high = combine.astype(jnp.bfloat16)
     rest = combine - high.astype(jnp.float32)
@@ -314,20 +360,20 @@
         + jnp.dot(high, answers, preferred_element_type=jnp.float32)
     ).astype(jnp.bfloat16)
 
-    each(
-        1, groups,
-        lambda o: spread(
-            outgoing, arrived, out_send, out_recv, o, lax.rem(me + o, groups)
-        ).wait_send(),
-    )
-    each(
-        1, groups,
-        lambda o: spread(
-            leaving, returned, ret_send, ret_recv, o, lax.rem(me + o, groups)
-        ).wait_send(),
-    )
+    blocks(outgoing, arrived, out_send, out_recv).wait_send()
+    blocks(leaving, returned, ret_send, ret_recv).wait_send()
     each(1, n, lambda o: part_copy(o).wait_send())
     each(1, n, lambda o: hidden_copy(o, p).wait_send())
+    if tilt:
+
+        @pl.when(p == 0)
+        def _():
+            tilt_part.wait_send()
+
+        @pl.when(p == 1)
+        def _():
+            tilt_hidden.wait_send()
+
 
     def finish(i):
         sync_copy(i).wait_send()
@@ -376,7 +422,6 @@
     p, me = lax.axis_index("dp"), lax.axis_index("expert")
     width = wide.shape[2]
     first = (n - 1) * el * nsub - late
-    stop = lax.rem(me, 2) * late
 
     def load(i):
         offset, e, r = chunk_at(dims, first + i)
@@ -401,17 +446,19 @@
         narrow[i] = wide[i].astype(jnp.bfloat16)
         copy(i).start()
 
-    barrier = pltpu.get_barrier_semaphore()
-    each(
-        1, n,
-        lambda o: pl.semaphore_signal(
-            barrier, inc=1, device_id=(lax.rem(p + o, n), me), device_id_type=MESH
-        ),
-    )
-    each(0, stop, lambda i: load(i).start())
-    pl.semaphore_wait(barrier, n - 1)
-    each(0, stop, send)
-    each(0, stop, lambda i: copy(i).wait())
+    @pl.when(lax.rem(me, 2) == 1)
+    def _():
+        barrier = pltpu.get_barrier_semaphore()
+        each(
+            1, n,
+            lambda o: pl.semaphore_signal(
+                barrier, inc=1, device_id=(lax.rem(p + o, n), me), device_id_type=MESH
+            ),
+        )
+        each(0, late, lambda i: load(i).start())
+        pl.semaphore_wait(barrier, n - 1)
+        each(0, late, send)
+        each(0, late, lambda i: copy(i).wait())
 
 
 def settle(dims, tail, stored, synced_out, sems):
@@ -438,7 +485,8 @@
     rows = trained_down.shape[1]
     slots = el * CAP
     total = groups * slots
-    share = total // n
+    tilt = tilt_of(n, total)
+    share = (total - tilt) // n
     fits = [
         d for d in range(16, rows + 1, 16) if rows % d == 0 and d * width * 2 <= CHUNK_BYTES
     ]
@@ -472,7 +520,8 @@
             pltpu.VMEM(gate_weight.shape, bf16),
             pltpu.VMEM(up_weight.shape, bf16),
             pltpu.VMEM(down_weight.shape, bf16),
-            pltpu.VMEM((chunks, rc, width), f32),
+            pltpu.VMEM((remote, rc, width), f32),
+            pltpu.VMEM((el, rows, width), f32),
             pltpu.VMEM((remote, rc, width), bf16),
             pltpu.VMEM((groups, slots, width), bf16),
             pltpu.VMEM((groups, slots, width), bf16),
@@ -480,22 +529,26 @@
             pltpu.VMEM((total, 2 * ff), f32),
             pltpu.VMEM((n, share, 2 * ff), bf16),
             pltpu.VMEM((n, share, 2 * ff), bf16),
+            pltpu.VMEM((max(tilt, 16), 2 * ff), bf16),
+            pltpu.VMEM((max(tilt, 16), 2 * ff), bf16),
             pltpu.VMEM((total, ff), bf16),
             pltpu.VMEM((groups, slots, width), bf16),
             pltpu.VMEM((groups, slots, width), bf16),
             dma((3,)),
             dma((3 * el,)),
-            dma((chunks,)),
+            dma((remote,)),
+            dma(()),
             dma((remote,)),
             dma((remote,)),
-            dma((groups,)),
-            dma((groups,)),
+            dma(()),
+            dma(()),
             dma((n,)),
             dma((n,)),
             dma((n,)),
             dma((n,)),
-            dma((groups,)),
-            dma((groups,)),
+            dma(()),
+            dma(()),
+            dma((4,)),
             pltpu.SemaphoreType.REGULAR,
             pltpu.SemaphoreType.REGULAR,
         ],

time: 85.9 us -> 85.4 us (level)
    pallas_call x1, Pallas kernels: 71.5 us -> 70.3 us  [local(): pl.pallas_call(functools.partial(fused, dims), out_shape=(pltpu.VMEM((tok...]
where the time goes in v3:
time: 85.4 us; the launch traced here: 85.2 us
  Pallas kernels  84.6 us (99%)
    pallas_call x1, Pallas kernels, local(): pl.pallas_call(functools.partial(fused, dims), out_shape=(pltpu.VMEM((tok...  70.3 us
    pallas_call x1, Pallas kernels, local(): pl.pallas_call(functools.partial(trailing, dims), out_shape=pltpu.VMEM((l...  10.7 us
    pallas_call x1, Pallas kernels, local(): pl.pallas_call(functools.partial(store, dims), out_shape=(jax.ShapeDtypeS...  2.67 us

profile of v3, /device:TPU:1, one launch (start us, length us, event | category | flops | bytes accessed | tf_op | source)
XLA Modules:
  0.0 85.2 jit_solution(6113601733300026694)
XLA Ops:
  0.6 70.3 %shard_map.86 = (bf16[32,1024]{1,0:T(8,128)(2,1)S(1)}, bf16[4,768,1024]{2,1,0:T(8,128)(2,1)S(1)}) custom-call(bf16[32,1024]{1,0:T(8,128)(2,1)} %tokens.1, s32[8,32]{1,0:T(8,128)} %bitcast.2, f32[8,32]{1,0:T(8,128)} %bitcast.3, bf16[4,1024,768]{2,1,0:T(8,128)(2,1)} %gate_weight.1, bf16[4,1024,768]{2,1,0:T(8,128)(2,1)} %up_weight.1, ...), custom_call_target="tpu_custom_call" | custom-call | flops 1207959552 | bytes 268435456 | tf_op jit(solution)/shard_map/pallas_call | solution.py:508
  71.0 2.7 %shard_map.87 = (bf16[32,1024]{1,0:T(8,128)(2,1)}, bf16[4,768,1024]{2,1,0:T(8,128)(2,1)}, f32[8,128]{1,0:T(8,128)S(1)}) custom-call(bf16[32,1024]{1,0:T(8,128)(2,1)S(1)} %get-tuple-element.7.mixed, bf16[4,768,1024]{2,1,0:T(8,128)(2,1)S(1)} %get-tuple-element.8.synced), custom_call_target="tpu_custom_call" | custom-call | tf_op jit(solution)/shard_map/pallas_call | solution.py:562
  73.6 10.7 %shard_map.88.tail = bf16[3,96,1024]{2,1,0:T(8,128)(2,1)S(1)} custom-call(f32[4,384,2048]{2,1,0:T(8,128)} %trained.3, f32[8,128]{1,0:T(8,128)S(1)} %get-tuple-element.10.mark), custom_call_target="tpu_custom_call" | custom-call | tf_op jit(solution)/shard_map/pallas_call | solution.py:574
  84.4 0.9 %shard_map.89 = bf16[4,768,1024]{2,1,0:T(8,128)(2,1)} custom-call(bf16[3,96,1024]{2,1,0:T(8,128)(2,1)S(1)} %shard_map.88.tail, bf16[4,768,1024]{2,1,0:T(8,128)(2,1)} %get-tuple-element.11.stored), custom_call_target="tpu_custom_call", output_to_operand_aliasing={{}: (1, {})} | custom-call | tf_op jit(solution)/shard_map/pallas_call | solution.py:590

commit v4 on v3

--- a/solution.py
+++ b/solution.py
@@ -229,7 +229,7 @@
     def _():
         pl.semaphore_signal(entered, inc=1, device_id=(p, me + 1), device_id_type=MESH)
 
-    each(0, FIRST, send_chunk)
+    each(0, early, send_chunk)
 
     for copy in smalls:
         copy.wait()
@@ -260,7 +260,6 @@
         pl.semaphore_wait(entered, 1)
 
     spread_all(outgoing, arrived, out_send, out_recv)
-    each(FIRST, early, send_chunk)
 
     r = lax.broadcasted_iota(jnp.int32, (total, total), 0)
     c = lax.broadcasted_iota(jnp.int32, (total, total), 1)
@@ -435,8 +434,8 @@
         return pltpu.make_async_remote_copy(
             src_ref=narrow.at[i],
             dst_ref=tail.at[i],
-            send_sem=send_sem.at[i],
-            recv_sem=recv_sem.at[i],
+            send_sem=send_sem,
+            recv_sem=recv_sem,
             device_id=(lax.rem(p + offset, n), me),
             device_id_type=MESH,
         )
@@ -458,7 +457,14 @@
         each(0, late, lambda i: load(i).start())
         pl.semaphore_wait(barrier, n - 1)
         each(0, late, send)
-        each(0, late, lambda i: copy(i).wait())
+        pltpu.make_async_remote_copy(
+            src_ref=narrow,
+            dst_ref=tail,
+            send_sem=send_sem,
+            recv_sem=recv_sem,
+            device_id=(lax.rem(p + 1, n), me),
+            device_id_type=MESH,
+        ).wait()
 
 
 def settle(dims, tail, stored, synced_out, sems):
@@ -580,8 +586,8 @@
             pltpu.VMEM((late, rc, width), f32),
             pltpu.VMEM((late, rc, width), bf16),
             dma((late,)),
-            dma((late,)),
-            dma((late,)),
+            dma(()),
+            dma(()),
         ],
         compiler_params=pltpu.CompilerParams(
             collective_id=1, has_side_effects=True, vmem_limit_bytes=56 * 2**20

time: 85.4 us -> 85.3 us (level)
  no operation moved by 1% of the time
where the time goes in v4:
time: 85.3 us; the launch traced here: 85.1 us
  Pallas kernels  84.5 us (99%)
    pallas_call x1, Pallas kernels, local(): pl.pallas_call(functools.partial(fused, dims), out_shape=(pltpu.VMEM((tok...  70.2 us
    pallas_call x1, Pallas kernels, local(): pl.pallas_call(functools.partial(trailing, dims), out_shape=pltpu.VMEM((l...  10.7 us
    pallas_call x1, Pallas kernels, local(): pl.pallas_call(functools.partial(store, dims), out_shape=(jax.ShapeDtypeS...  2.67 us

profile of v4, /device:TPU:1, one launch (start us, length us, event | category | flops | bytes accessed | tf_op | source)
XLA Modules:
  0.0 85.1 jit_solution(10103244795896097176)
XLA Ops:
  0.6 70.2 %shard_map.86 = (bf16[32,1024]{1,0:T(8,128)(2,1)S(1)}, bf16[4,768,1024]{2,1,0:T(8,128)(2,1)S(1)}) custom-call(bf16[32,1024]{1,0:T(8,128)(2,1)} %tokens.1, s32[8,32]{1,0:T(8,128)} %bitcast.2, f32[8,32]{1,0:T(8,128)} %bitcast.3, bf16[4,1024,768]{2,1,0:T(8,128)(2,1)} %gate_weight.1, bf16[4,1024,768]{2,1,0:T(8,128)(2,1)} %up_weight.1, ...), custom_call_target="tpu_custom_call" | custom-call | flops 1207959552 | bytes 268435456 | tf_op jit(solution)/shard_map/pallas_call | solution.py:514
  70.9 2.7 %shard_map.87 = (bf16[32,1024]{1,0:T(8,128)(2,1)}, bf16[4,768,1024]{2,1,0:T(8,128)(2,1)}, f32[8,128]{1,0:T(8,128)S(1)}) custom-call(bf16[32,1024]{1,0:T(8,128)(2,1)S(1)} %get-tuple-element.7.mixed, bf16[4,768,1024]{2,1,0:T(8,128)(2,1)S(1)} %get-tuple-element.8.synced), custom_call_target="tpu_custom_call" | custom-call | tf_op jit(solution)/shard_map/pallas_call | solution.py:568
  73.5 10.7 %shard_map.88.tail = bf16[3,96,1024]{2,1,0:T(8,128)(2,1)S(1)} custom-call(f32[4,384,2048]{2,1,0:T(8,128)} %trained.3, f32[8,128]{1,0:T(8,128)S(1)} %get-tuple-element.10.mark), custom_call_target="tpu_custom_call" | custom-call | tf_op jit(solution)/shard_map/pallas_call | solution.py:580
  84.2 0.9 %shard_map.89 = bf16[4,768,1024]{2,1,0:T(8,128)(2,1)} custom-call(bf16[3,96,1024]{2,1,0:T(8,128)(2,1)S(1)} %shard_map.88.tail, bf16[4,768,1024]{2,1,0:T(8,128)(2,1)} %get-tuple-element.11.stored), custom_call_target="tpu_custom_call", output_to_operand_aliasing={{}: (1, {})} | custom-call | tf_op jit(solution)/shard_map/pallas_call | solution.py:596

commit v5 on v4

--- a/solution.py
+++ b/solution.py
@@ -9,7 +9,7 @@
 
 CAP = 4
 CHUNK_BYTES = 200_000
-FIRST = 2
+FIRST = 1
 EARLY = 5 / 16
 MIDDLE = 1 / 16
 LATE = 3 / 16
@@ -69,6 +69,7 @@
     early = round(remote * EARLY)
     middle = early + round(remote * MIDDLE)
     own = remote - core * late
+    cover = min(COVER, remote - late)
 
     def peer(offset):
         return lax.rem(p + offset, n)
@@ -378,13 +379,13 @@
         sync_copy(i).wait_send()
         sync_arrival(i).wait_recv()
 
-    each(0, own - COVER, finish)
+    each(0, own - cover, finish)
 
     @pl.when(core == 0)
     def _():
         pl.semaphore_signal(nearly, inc=1, device_id=(p, me + 1), device_id_type=MESH)
 
-    each(own - COVER, own, finish)
+    each(own - cover, own, finish)
 
     @pl.when(core == 1)
     def _():

time: 85.3 us -> 85.2 us (level)
  no operation moved by 1% of the time
where the time goes in v5:
time: 85.2 us; the launch traced here: 85.1 us
  Pallas kernels  84.4 us (99%)
    pallas_call x1, Pallas kernels, local(): pl.pallas_call(functools.partial(fused, dims), out_shape=(pltpu.VMEM((tok...  70.2 us
    pallas_call x1, Pallas kernels, local(): pl.pallas_call(functools.partial(trailing, dims), out_shape=pltpu.VMEM((l...  10.7 us
    pallas_call x1, Pallas kernels, local(): pl.pallas_call(functools.partial(store, dims), out_shape=(jax.ShapeDtypeS...  2.67 us

profile of v5, /device:TPU:1, one launch (start us, length us, event | category | flops | bytes accessed | tf_op | source)
XLA Modules:
  0.0 85.1 jit_solution(15054746687428004280)
XLA Ops:
  0.6 70.2 %shard_map.86 = (bf16[32,1024]{1,0:T(8,128)(2,1)S(1)}, bf16[4,768,1024]{2,1,0:T(8,128)(2,1)S(1)}) custom-call(bf16[32,1024]{1,0:T(8,128)(2,1)} %tokens.1, s32[8,32]{1,0:T(8,128)} %bitcast.2, f32[8,32]{1,0:T(8,128)} %bitcast.3, bf16[4,1024,768]{2,1,0:T(8,128)(2,1)} %gate_weight.1, bf16[4,1024,768]{2,1,0:T(8,128)(2,1)} %up_weight.1, ...), custom_call_target="tpu_custom_call" | custom-call | flops 1207959552 | bytes 268435456 | tf_op jit(solution)/shard_map/pallas_call | solution.py:515
  70.9 2.7 %shard_map.87 = (bf16[32,1024]{1,0:T(8,128)(2,1)}, bf16[4,768,1024]{2,1,0:T(8,128)(2,1)}, f32[8,128]{1,0:T(8,128)S(1)}) custom-call(bf16[32,1024]{1,0:T(8,128)(2,1)S(1)} %get-tuple-element.7.mixed, bf16[4,768,1024]{2,1,0:T(8,128)(2,1)S(1)} %get-tuple-element.8.synced), custom_call_target="tpu_custom_call" | custom-call | tf_op jit(solution)/shard_map/pallas_call | solution.py:569
  73.5 10.7 %shard_map.88.tail = bf16[3,96,1024]{2,1,0:T(8,128)(2,1)S(1)} custom-call(f32[4,384,2048]{2,1,0:T(8,128)} %trained.3, f32[8,128]{1,0:T(8,128)S(1)} %get-tuple-element.10.mark), custom_call_target="tpu_custom_call" | custom-call | tf_op jit(solution)/shard_map/pallas_call | solution.py:581
  84.2 0.9 %shard_map.89 = bf16[4,768,1024]{2,1,0:T(8,128)(2,1)} custom-call(bf16[3,96,1024]{2,1,0:T(8,128)(2,1)S(1)} %shard_map.88.tail, bf16[4,768,1024]{2,1,0:T(8,128)(2,1)} %get-tuple-element.11.stored), custom_call_target="tpu_custom_call", output_to_operand_aliasing={{}: (1, {})} | custom-call | tf_op jit(solution)/shard_map/pallas_call | solution.py:597

commit v6 on v5

--- a/solution.py
+++ b/solution.py
@@ -8,12 +8,12 @@
 from jax.sharding import PartitionSpec as P
 
 CAP = 4
-CHUNK_BYTES = 200_000
+CHUNK_BYTES = 150_000
 FIRST = 1
 EARLY = 5 / 16
 MIDDLE = 1 / 16
 LATE = 3 / 16
-COVER = 4
+COVER = 6
 TILT = 8
 MESH = pl.DeviceIdType.MESH
 

time: 85.2 us -> 85.2 us (level)
    pallas_call x1, Pallas kernels: 10.7 us -> 9.7 us  [local(): pl.pallas_call(functools.partial(trailing, dims), out_shape=pltpu.VMEM((l...]
    pallas_call x1, Pallas kernels: 70.2 us -> 71.1 us  [local(): pl.pallas_call(functools.partial(fused, dims), out_shape=(pltpu.VMEM((tok...]
where the time goes in v6:
time: 85.2 us; the launch traced here: 85 us
  Pallas kernels  84.4 us (99%)
    pallas_call x1, Pallas kernels, local(): pl.pallas_call(functools.partial(fused, dims), out_shape=(pltpu.VMEM((tok...  71.1 us
    pallas_call x1, Pallas kernels, local(): pl.pallas_call(functools.partial(trailing, dims), out_shape=pltpu.VMEM((l...  9.7 us
    pallas_call x1, Pallas kernels, local(): pl.pallas_call(functools.partial(store, dims), out_shape=(jax.ShapeDtypeS...  2.75 us

profile of v6, /device:TPU:1, one launch (start us, length us, event | category | flops | bytes accessed | tf_op | source)
XLA Modules:
  0.0 85.0 jit_solution(15767715461988700577)
XLA Ops:
  0.6 71.1 %shard_map.86 = (bf16[32,1024]{1,0:T(8,128)(2,1)S(1)}, bf16[4,768,1024]{2,1,0:T(8,128)(2,1)S(1)}) custom-call(bf16[32,1024]{1,0:T(8,128)(2,1)} %tokens.1, s32[8,32]{1,0:T(8,128)} %bitcast.2, f32[8,32]{1,0:T(8,128)} %bitcast.3, bf16[4,1024,768]{2,1,0:T(8,128)(2,1)} %gate_weight.1, bf16[4,1024,768]{2,1,0:T(8,128)(2,1)} %up_weight.1, ...), custom_call_target="tpu_custom_call" | custom-call | flops 1207959552 | bytes 268435456 | tf_op jit(solution)/shard_map/pallas_call | solution.py:515
  71.7 2.7 %shard_map.87 = (bf16[32,1024]{1,0:T(8,128)(2,1)}, bf16[4,768,1024]{2,1,0:T(8,128)(2,1)}, f32[8,128]{1,0:T(8,128)S(1)}) custom-call(bf16[32,1024]{1,0:T(8,128)(2,1)S(1)} %get-tuple-element.7.mixed, bf16[4,768,1024]{2,1,0:T(8,128)(2,1)S(1)} %get-tuple-element.8.synced), custom_call_target="tpu_custom_call" | custom-call | tf_op jit(solution)/shard_map/pallas_call | solution.py:569
  74.5 9.7 %shard_map.88.tail = bf16[4,64,1024]{2,1,0:T(8,128)(2,1)S(1)} custom-call(f32[4,384,2048]{2,1,0:T(8,128)} %trained.3, f32[8,128]{1,0:T(8,128)S(1)} %get-tuple-element.10.mark), custom_call_target="tpu_custom_call" | custom-call | tf_op jit(solution)/shard_map/pallas_call | solution.py:581
  84.2 0.8 shard_map.89
